TPU v7x, 32 devices: a whole 2x2x4 slice. The times are simulated.
32 devices in a mesh: node: 8 (over z, x), expert: 4 (over y, core).
Axes of the slice: x: 2, y: 2, z: 4, core: 2. Of those that a mesh axis runs over, the one named last changes fastest.
Arguments:
- tokens: bfloat16 [16384, 1024], P(('node', 'expert')), may hold values from -6 to 6
- queries: bfloat16 [16384, 1024], P(('node', 'expert')), may hold values from -6 to 6
- keys: bfloat16 [16384, 1024], P(('node', 'expert')), may hold values from -6 to 6
- values: bfloat16 [16384, 1024], P(('node', 'expert')), may hold values from -12 to 12
- neighbours: int32 [128, 8], P(('node', 'expert')), may hold values from 0 to 127, as said below
- live_bits: int32 [128, 8], P(('node', 'expert')), may hold values from 0 to 1, as said below
- out_proj: bfloat16 [1024, 1024], replicated, may hold values from -0.1875 to 0.1875
- norm_gain: float32 [1024], replicated, may hold values from 0.5 to 1.5
- router: bfloat16 [1024, 32], replicated, may hold values from -0.1875 to 0.1875
- expert: int32 [16384], P(('node', 'expert')), may hold values from 0 to 31, as said below
- slot: int32 [16384], P(('node', 'expert')), may hold values from 0 to 31, as said below
- w_up: bfloat16 [32, 1024, 4096], P(('node', 'expert')), may hold values from -0.1875 to 0.1875
- w_down: bfloat16 [32, 4096, 1024], P(('node', 'expert')), may hold values from -0.09375 to 0.09375
Outputs:
- layer_out: bfloat16 [16384, 1024], P(('node', 'expert'))
Inputs may be any that keep to these rules, and one draw needn't show every extreme that they name: Tile g is held by device g // 4 in node-major order. neighbours[g, 0] is g itself; every listed tile is held by g's device or by the device one step before or after it along node with the same expert index (wrapping around); entry 1 is always one step before and entry 2 one step after. `live_bits`: entry 0 of every row is 1. Within the 512 tokens of one device, no two tokens share both expert and slot; some expert takes all 32 slots of every device. See expert: pairs (expert, slot) are distinct within one device's tokens.
All inputs are finite; a program needn't handle non-finite values.
Results may differ from a plain program's by a relative error of at most 0.0049.
Values may be sent and summed in bfloat16 or wider, within the bound.
A program may use at most 192 MiB of HBM per device.

v0:
```python
import jax
import jax.numpy as jnp
from jax import lax
from jax.sharding import PartitionSpec as P

D = 1024
HEADS = 16
HEAD_DIM = 64
TILE = 128
NB = 8


score_scale = 0.125


def extended(shard, sides, width):
    for axis, dim in sides:
        size, length = (lax.axis_size(axis), shard.shape[dim])
        up = [(i, (i + 1) % size) for i in range(size)]
        down = [(j, i) for i, j in up]
        last = lax.slice_in_dim(shard, length - width, length, axis=dim)
        leading = lax.slice_in_dim(shard, 0, width, axis=dim)
        before = lax.ppermute(last, axis, up)
        after = lax.ppermute(leading, axis, down)
        shard = jnp.concatenate([before, shard, after], axis=dim)
    return shard


def shards(
    tokens,
    queries,
    keys,
    values,
    neighbours,
    live_bits,
    out_proj,
    norm_gain,
    router,
    expert,
    slot,
    w_up,
    w_down,
):
    tok_dev = tokens.shape[0]
    tiles_dev = tok_dev // TILE
    experts = router.shape[1]
    cap = 2 * tok_dev // experts
    both = jnp.concatenate([keys, values], axis=1)
    widened = extended(both, (("node", 0),), tok_dev)
    window_tiles = widened.reshape(3 * tiles_dev, TILE, 2 * D)
    my_node = lax.axis_index("node")
    node_count = lax.axis_size("node")
    column_count = lax.axis_size("expert")
    owner_node = neighbours // tiles_dev // column_count
    offset = (owner_node - my_node + node_count) % node_count
    block_of = jnp.where(offset == 0, 1, jnp.where(offset == 1, 2, 0))
    position = block_of * tiles_dev + neighbours % tiles_dev
    gathered = window_tiles[position]
    near_keys = gathered[..., :D].reshape(tiles_dev, NB * TILE, HEADS, HEAD_DIM)
    near_values = gathered[..., D:].reshape(tiles_dev, NB * TILE, HEADS, HEAD_DIM)
    query_tiles = queries.reshape(tiles_dev, TILE, HEADS, HEAD_DIM)
    scores = (
        jnp.einsum("tqhd,tkhd->thqk", query_tiles, near_keys, preferred_element_type=jnp.float32)
        * score_scale
    )
    visible = jnp.repeat(live_bits, TILE, axis=1) > 0
    masked = jnp.where(visible[:, None, None, :], scores, -jnp.inf)
    peak = jnp.max(masked, axis=-1, keepdims=True)
    weights = jnp.exp(masked - peak)
    weights = (weights / jnp.sum(weights, axis=-1, keepdims=True)).astype(jnp.bfloat16)
    mixed = jnp.einsum("thqk,tkhd->tqhd", weights, near_values, preferred_element_type=jnp.float32)
    attn = mixed.reshape(tok_dev, D).astype(jnp.bfloat16)
    hidden = tokens.astype(jnp.float32) + jnp.dot(
        attn, out_proj, preferred_element_type=jnp.float32
    )
    spread = jnp.mean(hidden * hidden, axis=-1, keepdims=True)
    normed = (hidden * lax.rsqrt(spread + 1e-06) * norm_gain[None, :]).astype(jnp.bfloat16)
    logits = jnp.dot(normed, router, preferred_element_type=jnp.float32)
    columns = lax.iota(jnp.int32, experts)
    chosen = jnp.sum(jnp.where(columns[None, :] == expert[:, None], logits, 0.0), axis=-1)
    gate = jax.nn.sigmoid(chosen)
    slot_cell = expert * cap + slot
    one_hot = (lax.iota(jnp.int32, experts * cap)[:, None] == slot_cell[None, :]).astype(
        jnp.bfloat16
    )
    outgoing = jnp.dot(one_hot, normed, preferred_element_type=jnp.float32).astype(jnp.bfloat16)
    up_matrix = w_up[0]
    down_matrix = w_down[0]
    block = lax.all_to_all(
        outgoing.reshape(experts, 1, cap, D),
        ("node", "expert"),
        split_axis=0,
        concat_axis=1,
        tiled=True,
    )
    token_rows = block.reshape(-1, D)
    lifted = jnp.dot(token_rows, up_matrix, preferred_element_type=jnp.float32)
    lifted = jax.nn.gelu(lifted, approximate=True).astype(jnp.bfloat16)
    result = jnp.dot(lifted, down_matrix, preferred_element_type=jnp.float32).astype(jnp.bfloat16)
    returned = lax.all_to_all(
        result.reshape(block.shape), ("node", "expert"), split_axis=1, concat_axis=0, tiled=True
    )
    flat_back = returned.reshape(experts * cap, D)
    expert_out = jnp.einsum("ct,cd->td", one_hot, flat_back, preferred_element_type=jnp.float32)
    layer_out = hidden + gate[:, None] * expert_out
    return layer_out.astype(jnp.bfloat16)


def solution(mesh):
    in_specs = (
        P(("node", "expert"), None),
        P(("node", "expert"), None),
        P(("node", "expert"), None),
        P(("node", "expert"), None),
        P(("node", "expert"), None),
        P(("node", "expert"), None),
        P(),
        P(),
        P(),
        P(("node", "expert")),
        P(("node", "expert")),
        P(("node", "expert"), None, None),
        P(("node", "expert"), None, None),
    )
    out_specs = P(("node", "expert"), None)
    return jax.shard_map(shards, mesh=mesh, in_specs=in_specs, out_specs=out_specs, check_vma=False)
```

profile of v0, /device:TPU:0, one launch (start us, length us, event | category | flops | bytes accessed | tf_op | source)
XLA Modules:
  0.0 354.1 jit_solution(12946120193367616058)
XLA Ops:
  0.0 2.5 constant_dynamic-update-slice_fusion.1
  2.5 2.3 constant_dynamic-update-slice_fusion
  4.8 6.0 %collective-permute-start.1 = (bf16[512,2048]{1,0:T(8,128)(2,1)}, bf16[512,2048]{1,0:T(8,128)(2,1)}, u32[]{:S(2)}, u32[]{:S(2)}) collective-permute-start(bf16[512,2048]{1,0:T(8,128)(2,1)} %constant_dynamic-update-slice_fusion), channel_id=1, source_target_pairs={{4,0},{8,4},{12,8},{16,12},{20,16},{24,20},{28,24},{0,28},{5,1},{9... | collective-permute-start | bytes 6291464 | tf_op jit(solution)/shard_map/ppermute | solution.py:24
  12.3 4.0 %reshape.79 = bf16[4,128,16,64]{3,2,1,0:T(8,128)(2,1)} reshape(bf16[512,1024]{1,0:T(8,128)(2,1)} %param.14) | data formatting | bytes 2097152 | tf_op jit(solution)/shard_map/reshape | solution.py:61
  16.4 82.2 %collective-permute-done.1 = bf16[512,2048]{1,0:T(8,128)(2,1)} collective-permute-done((bf16[512,2048]{1,0:T(8,128)(2,1)}, bf16[512,2048]{1,0:T(8,128)(2,1)}, u32[]{:S(2)}, u32[]{:S(2)}) %collective-permute-start.1) | collective-permute-done | bytes 2097184 | tf_op jit(solution)/shard_map/ppermute | solution.py:24
  98.8 5.9 %pad_maximum_fusion = bf16[1536,2048]{1,0:T(8,128)(2,1)} fusion(bf16[512,2048]{1,0:T(8,128)(2,1)} %collective-permute-done.1, bf16[512,2048]{1,0:T(8,128)(2,1)} %constant_dynamic-update-slice_fusion, bf16[512,2048]{1,0:T(8,128)(2,1)} %collective-permute-done), kind=kLoop, calls=%fused_computation.28 | loop fusion | flops 18874368 | bytes 12582912 | tf_op jit(solution)/shard_map/concatenate | solution.py:25
  104.7 10.0 %gather_fusion = bf16[32,128,2048]{2,1,0:T(8,128)(2,1)} fusion(bf16[12,128,2048]{2,1,0:T(8,128)(2,1)} %bitcast.64, s32[1024]{0:T(1024)S(1)} %pad_clamp_fusion), kind=kCustom, calls=%fused_computation | custom fusion | bytes 33554560 | tf_op jit(solution)/shard_map/gather | solution.py:58
  114.7 11.9 %fusion.66 = (bf16[4,8,128,1024]{3,2,1,0:T(8,128)(2,1)}, bf16[4,8,128,1024]{3,2,1,0:T(8,128)(2,1)}) fusion(bf16[4,8,128,2048]{3,2,1,0:T(8,128)(2,1)} %bitcast.65), kind=kLoop, calls=%fused_computation.88 | loop fusion | bytes 33554432 | tf_op jit(solution)/shard_map/slice | solution.py:59
  126.6 12.3 %copy.22 = bf16[4,8,128,1024]{2,1,3,0:T(8,128)(2,1)} copy(bf16[4,8,128,1024]{3,2,1,0:T(8,128)(2,1)} %get-tuple-element.6) | data formatting | bytes 16777216 | tf_op jit(solution)/shard_map/slice | solution.py:60
  138.9 13.3 %reshape.62 = bf16[4,1024,16,64]{1,3,2,0:T(8,128)(2,1)} reshape(bf16[4,8,128,1024]{2,1,3,0:T(8,128)(2,1)} %copy.22) | data formatting | bytes 16777216 | tf_op jit(solution)/shard_map/reshape | solution.py:60
  152.2 12.3 %copy.23 = bf16[4,8,128,1024]{2,1,3,0:T(8,128)(2,1)} copy(bf16[4,8,128,1024]{3,2,1,0:T(8,128)(2,1)} %get-tuple-element.5) | data formatting | bytes 16777216 | tf_op jit(solution)/shard_map/slice | solution.py:59
  164.5 13.3 %reshape.63 = bf16[4,1024,16,64]{1,3,2,0:T(8,128)(2,1)} reshape(bf16[4,8,128,1024]{2,1,3,0:T(8,128)(2,1)} %copy.23) | data formatting | bytes 16777216 | tf_op jit(solution)/shard_map/reshape | solution.py:59
  177.8 18.8 %fusion.67 = (f32[4,16,128]{2,1,0:T(8,128)S(1)}, f32[4,16,128,1024]{2,3,1,0:T(8,128)}) fusion(pred[4,1024]{1,0:T(4,128)(4,1)S(1)} %bitcast.69, bf16[4,1024,16,64]{1,3,2,0:T(8,128)(2,1)} %reshape.63, bf16[4,128,16,64]{3,2,1,0:T(8,128)(2,1)} %reshape.79), kind=kOutput, calls=%fused_computation.89 | convolution fusion | flops 1107297280 | bytes 43028480 | tf_op jit(solution)/shard_map/sub | solution.py:69
  196.6 14.7 %fusion.47 = bf16[4,128,16,64]{1,3,2,0:T(8,128)(2,1)S(1)} fusion(bf16[4,1024,16,64]{1,3,2,0:T(8,128)(2,1)} %reshape.62, f32[4,16,128,1024]{2,3,1,0:T(8,128)} %get-tuple-element.8, f32[4,16,128]{2,1,0:T(8,128)S(1)} %get-tuple-element.7), kind=kOutput, calls=%fused_computation.43 | convolution fusion | flops 1091043328 | bytes 43024384 | tf_op jit(solution)/shard_map/thqk,tkhd->tqhd/dot_general | solution.py:71
  211.2 0.9 copy.27
  212.1 2.6 multiply_reduce_fusion
  214.8 1.3 copy-done.2
  216.1 1.4 fusion.38
  217.5 54.7 %all_to_all.8 = bf16[32,1,32,1024]{3,2,1,0:T(8,128)(2,1)S(1)} all-to-all(bf16[32,1,32,1024]{3,2,1,0:T(8,128)(2,1)S(1)} %bitcast.68), channel_id=1, replica_groups=mesh['node'=8,'expert'=4] {'node','expert'}, dimensions={0} | all-to-all | bytes 4194304 | tf_op jit(solution)/shard_map/all_to_all | solution.py:89
  272.1 25.0 %fusion.29 = bf16[1024,1024]{1,0:T(8,128)(2,1)} fusion(bf16[1,4096,1024]{2,1,0:T(8,128)(2,1)} %param.25, bf16[1024,1024]{1,0:T(8,128)(2,1)S(1)} %bitcast.67, bf16[1,1024,4096]{2,1,0:T(8,128)(2,1)} %param.24), kind=kOutput, calls=%fused_computation.37 | convolution fusion | flops 17218666496 | bytes 20971520 | tf_op jit(solution)/shard_map/dot_general | solution.py:99
  297.1 3.8 %all-to-all-start.1 = ((bf16[1,32,32,1024]{3,2,0,1:T(8,128)(2,1)}), bf16[1,32,32,1024]{3,2,0,1:T(8,128)(2,1)}, u32[]{:S(2)}, u32[]{:S(2)}) async-start(bf16[1,32,32,1024]{3,2,0,1:T(8,128)(2,1)} %bitcast.10), calls=%async_computation.1 | async-start | bytes 4194304 | tf_op jit(solution)/shard_map/all_to_all | solution.py:100
  301.0 2.2 fusion.48
  303.2 46.4 %all-to-all-done.1 = bf16[1,32,32,1024]{3,2,0,1:T(8,128)(2,1)} async-done(((bf16[1,32,32,1024]{3,2,0,1:T(8,128)(2,1)}), bf16[1,32,32,1024]{3,2,0,1:T(8,128)(2,1)}, u32[]{:S(2)}, u32[]{:S(2)}) %all-to-all-start.1) | async-done | bytes 2097184 | tf_op jit(solution)/shard_map/all_to_all | solution.py:100
  349.6 4.5 %add_convert_fusion = bf16[512,1024]{1,0:T(8,128)(2,1)} fusion(f32[512,1024]{1,0:T(8,128)} %copy-done.2, bf16[1024,1024]{1,0:T(8,128)(2,1)} %bitcast.11, s32[512]{0:T(512)S(1)} %multiply_add_fusion, f32[512]{0:T(512)S(1)} %add_divide_fusion), kind=kOutput, calls=%fused_computation.30 | convolution fusion | flops 1075838976 | bytes 5246976 | tf_op jit(solution)/shard_map/ct,cd->td/dot_general | solution.py:104
  (26 shorter events, 1.8 us)
Async XLA Ops:
  0.0 212.1 %copy-start = (bf16[1024,1024]{1,0:T(8,128)(2,1)S(1)}, bf16[1024,1024]{1,0:T(8,128)(2,1)}, u32[]{:S(2)}) copy-start(bf16[1024,1024]{1,0:T(8,128)(2,1)} %param.19) | copy-start | bytes 6291460
  0.0 16.4 %copy-start.7 = (s32[512]{0:T(512)S(1)}, s32[512]{0:T(512)}, u32[]{:S(2)}) copy-start(s32[512]{0:T(512)} %param.23) | copy-start | bytes 6148
  0.0 16.4 %copy-start.4 = (s32[512]{0:T(512)S(1)}, s32[512]{0:T(512)}, u32[]{:S(2)}) copy-start(s32[512]{0:T(512)} %param.22) | copy-start | bytes 6148
  4.8 93.9 %collective-permute-start.1 = (bf16[512,2048]{1,0:T(8,128)(2,1)}, bf16[512,2048]{1,0:T(8,128)(2,1)}, u32[]{:S(2)}, u32[]{:S(2)}) collective-permute-start(bf16[512,2048]{1,0:T(8,128)(2,1)} %constant_dynamic-update-slice_fusion), channel_id=1, source_target_pairs={{4,0},{8,4},{12,8},{16,12},{20,16},{24,20},{28,24},{0,28},{5,1},{9... | collective-permute-start | bytes 6291464 | tf_op jit(solution)/shard_map/ppermute | solution.py:24
  10.8 88.0 %collective-permute-start = (bf16[512,2048]{1,0:T(8,128)(2,1)}, bf16[512,2048]{1,0:T(8,128)(2,1)}, u32[]{:S(2)}, u32[]{:S(2)}) collective-permute-start(bf16[512,2048]{1,0:T(8,128)(2,1)} %constant_dynamic-update-slice_fusion), channel_id=1, source_target_pairs={{0,4},{4,8},{8,12},{12,16},{16,20},{20,24},{24,28},{28,0},{1,5},{5... | collective-permute-start | bytes 6291464 | tf_op jit(solution)/shard_map/ppermute | solution.py:23
  211.2 4.9 %copy-start.6 = (f32[1024]{0:T(1024)S(1)}, f32[1024]{0:T(1024)}, u32[]{:S(2)}) copy-start(f32[1024]{0:T(1024)} %param.20) | copy-start | bytes 12292
  214.8 1.3 copy-start.2
  272.1 28.8 %copy-start.3 = (bf16[1024,32]{0,1:T(8,128)(2,1)S(1)}, bf16[1024,32]{0,1:T(8,128)(2,1)}, u32[]{:S(2)}) copy-start(bf16[1024,32]{0,1:T(8,128)(2,1)} %param.21) | copy-start | bytes 196612
  272.1 28.8 %copy-start.5 = (s32[512]{0:T(512)S(1)}, s32[512]{0:T(512)}, u32[]{:S(2)}) copy-start(s32[512]{0:T(512)} %param.22) | copy-start | bytes 6148
  297.1 52.5 %all-to-all-start.1 = ((bf16[1,32,32,1024]{3,2,0,1:T(8,128)(2,1)}), bf16[1,32,32,1024]{3,2,0,1:T(8,128)(2,1)}, u32[]{:S(2)}, u32[]{:S(2)}) async-start(bf16[1,32,32,1024]{3,2,0,1:T(8,128)(2,1)} %bitcast.10), calls=%async_computation.1 | async-start | bytes 4194304 | tf_op jit(solution)/shard_map/all_to_all | solution.py:100
  300.9 53.2 %copy-start.1 = (bf16[1024,1024]{1,0:T(8,128)(2,1)S(1)}, bf16[1024,1024]{1,0:T(8,128)(2,1)}, u32[]{:S(2)}) copy-start(bf16[1024,1024]{1,0:T(8,128)(2,1)} %param.19) | copy-start | bytes 6291460
where the time goes:
time: 356 us; the launch traced here: 354 us
  waiting for transfers between devices  129 us (36%)
  local copies, waits for them, and re-layouts  84.3 us (24%)
  matrix products  69.1 us (19%)
  blocking collectives  54.7 us (15%)
  starting transfers between devices  9.8 us (3%)
  other arithmetic  7.34 us (2%)
    ppermute x1, waiting for transfers between devices, extended(): after = lax.ppermute(leading, axis, down)  82.2 us
    all_to_all x1, blocking collectives, shards(): lax.all_to_all(outgoing.reshape(experts, 1, cap, D), ('node', 'expert'),...  54.7 us
    all_to_all x1, waiting for transfers between devices, shards(): lax.all_to_all(result.reshape(block.shape), ('node', 'expert'), split_axi...  46.4 us
    dot_general x1, matrix products, shards(): jnp.dot(lifted, down_matrix, preferred_element_type=jnp.float32)  25 us
    slice x2, local copies, waits for them, and re-layouts, shards(): near_keys = gathered[..., :D].reshape(tiles_dev, NB * TILE, HEADS, HEAD_DIM)  24.2 us
    sub x1, matrix products, shards(): weights = jnp.exp(masked - peak)  18.8 us
    dot_general x1, matrix products, shards(): jnp.einsum('thqk,tkhd->tqhd', weights, near_values, preferred_element_typ...  14.7 us
    reshape x1, local copies, waits for them, and re-layouts, shards(): gathered[..., D:].reshape(tiles_dev, NB * TILE, HEADS, HEAD_DIM)  13.3 us
  transfers between devices with their start and end apart: 3, of which 3 were waited for; matrix products, arithmetic and copies ran while one was open for 2% of the time, Pallas kernels for 0%

commit v1 on v0

v1 whole, which is shorter than its diff:
```python
import functools

import jax
import jax.numpy as jnp
from jax import lax
from jax.experimental import pallas as pl
from jax.experimental.pallas import tpu as pltpu
from jax.sharding import PartitionSpec as P

D = 1024
HEADS = 16
HEAD_DIM = 64
TILE = 128
NB = 8


score_scale = 0.125


CHUNKS = 4
HIDE = -1e30


def attention_kernel(
    nodes,
    position_ref,
    bias_ref,
    query_ref,
    key_ref,
    value_ref,
    token_ref,
    proj_ref,
    gain_ref,
    hidden_ref,
    normed_ref,
    *scratch,
):
    key_windows, value_windows = scratch[:CHUNKS], scratch[CHUNKS : 2 * CHUNKS]
    own_sem, x_send, x_recv, z_send, z_recv, attn_ref = scratch[2 * CHUNKS :]
    node = lax.axis_index("node")
    odd = node % 2
    partner = node + 1 - 2 * odd
    onward = (node + 2 - 4 * odd + nodes) % nodes
    behind = (node - 2 + 4 * odd + nodes) % nodes
    tiles = key_windows[0].shape[0] // 3
    width = key_windows[0].shape[2]
    barrier = pltpu.get_barrier_semaphore()
    for other in (partner, onward, behind):
        pl.semaphore_signal(
            barrier, inc=1, device_id={"node": other}, device_id_type=pl.DeviceIdType.MESH
        )
    pl.semaphore_wait(barrier, 3)
    own, first, second = [], [], []
    for c in range(CHUNKS):
        columns = pl.ds(c * width, width)
        for s, (source, window) in enumerate(
            ((key_ref, key_windows[c]), (value_ref, value_windows[c]))
        ):
            block = source.at[:, :, columns]
            own.append(
                pltpu.make_async_copy(block, window.at[pl.ds(0, tiles)], own_sem.at[2 * c + s])
            )
            first.append(
                pltpu.make_async_remote_copy(
                    src_ref=block,
                    dst_ref=window.at[pl.ds(tiles, tiles)],
                    send_sem=x_send.at[2 * c + s],
                    recv_sem=x_recv.at[2 * c + s],
                    device_id={"node": partner},
                    device_id_type=pl.DeviceIdType.MESH,
                )
            )
            second.append(
                pltpu.make_async_remote_copy(
                    src_ref=window.at[pl.ds(tiles, tiles)],
                    dst_ref=window.at[pl.ds(2 * tiles, tiles)],
                    send_sem=z_send.at[2 * c + s],
                    recv_sem=z_recv.at[2 * c + s],
                    device_id={"node": onward},
                    device_id_type=pl.DeviceIdType.MESH,
                )
            )
    for copy in first:
        copy.start()
    for copy in own:
        copy.start()
    hidden_ref[...] = token_ref[...].astype(jnp.float32)
    heads = width // HEAD_DIM
    lane_head = lax.broadcasted_iota(jnp.int32, (TILE, width), 1) // HEAD_DIM

    def relay(c):
        for s in range(2):
            first[2 * c + s].wait_recv()
            second[2 * c + s].start()

    def attend(c):
        def one_tile(t, carry):
            rows = pl.ds(pl.multiple_of(t * TILE, TILE), TILE)
            query = query_ref[rows, c * width : (c + 1) * width] * jnp.bfloat16(score_scale)
            near_keys = jnp.concatenate(
                [key_windows[c][position_ref[t, j]] for j in range(NB)], axis=0
            )
            near_values = jnp.concatenate(
                [value_windows[c][position_ref[t, j]] for j in range(NB)], axis=0
            )
            bias = bias_ref[t]
            mixed = jnp.zeros((TILE, width), jnp.float32)
            for h in range(heads):
                mine = jnp.where(lane_head == h, query, jnp.zeros_like(query))
                scores = lax.dot_general(
                    mine,
                    near_keys,
                    (((1,), (1,)), ((), ())),
                    preferred_element_type=jnp.float32,
                )
                scores = scores + bias
                peak = jnp.max(scores, axis=-1, keepdims=True)
                weights = jnp.exp(scores - peak)
                share = 1.0 / jnp.sum(weights, axis=-1, keepdims=True)
                weights = (weights * share).astype(jnp.bfloat16)
                out = jnp.dot(weights, near_values, preferred_element_type=jnp.float32)
                mixed = jnp.where(lane_head == h, out, mixed)
            attn_ref[rows, :] = mixed.astype(jnp.bfloat16)
            return carry

        lax.fori_loop(0, tiles, one_tile, 0)

        def project(t, carry):
            rows = pl.ds(pl.multiple_of(t * TILE, TILE), TILE)
            hidden_ref[rows, :] += jnp.dot(
                attn_ref[rows, :],
                proj_ref[c * width : (c + 1) * width, :],
                preferred_element_type=jnp.float32,
            )
            return carry

        lax.fori_loop(0, tiles, project, 0)

    relay(0)
    for c in range(CHUNKS):
        if c + 1 < CHUNKS:
            relay(c + 1)
        for s in range(2):
            own[2 * c + s].wait()
            second[2 * c + s].wait_recv()
        attend(c)

    def finish(t, carry):
        rows = pl.ds(pl.multiple_of(t * TILE, TILE), TILE)
        hidden = hidden_ref[rows, :]
        spread = jnp.mean(hidden * hidden, axis=-1, keepdims=True)
        normed = hidden * lax.rsqrt(spread + 1e-06) * gain_ref[...]
        normed_ref[rows, :] = normed.astype(jnp.bfloat16)
        return carry

    lax.fori_loop(0, tiles, finish, 0)
    for copy in first + second:
        copy.wait_send()


def attention_block(tokens, queries, keys, values, position, live_bits, out_proj, norm_gain):
    tok_dev = tokens.shape[0]
    tiles = tok_dev // TILE
    width = D // CHUNKS
    bias = jnp.where(jnp.repeat(live_bits, TILE, axis=1) > 0, 0.0, HIDE).astype(jnp.float32)
    window = pltpu.VMEM((3 * tiles, TILE, width), jnp.bfloat16)
    sems = pltpu.SemaphoreType.DMA((2 * CHUNKS,))
    vmem = pl.BlockSpec(memory_space=pltpu.VMEM)
    return pl.pallas_call(
        functools.partial(attention_kernel, lax.axis_size("node")),
        out_shape=(
            jax.ShapeDtypeStruct((tok_dev, D), jnp.float32),
            jax.ShapeDtypeStruct((tok_dev, D), jnp.bfloat16),
        ),
        in_specs=[
            pl.BlockSpec(memory_space=pltpu.SMEM),
            vmem,
            vmem,
            pl.BlockSpec(memory_space=pl.ANY),
            pl.BlockSpec(memory_space=pl.ANY),
            vmem,
            vmem,
            vmem,
        ],
        out_specs=(vmem, vmem),
        scratch_shapes=[window] * (2 * CHUNKS)
        + [sems] * 5
        + [pltpu.VMEM((tok_dev, width), jnp.bfloat16)],
        compiler_params=pltpu.CompilerParams(
            collective_id=0, has_side_effects=True, vmem_limit_bytes=48 * 1024 * 1024
        ),
    )(
        position,
        bias.reshape(tiles, 1, NB * TILE),
        queries,
        keys.reshape(tiles, TILE, D),
        values.reshape(tiles, TILE, D),
        tokens,
        out_proj,
        norm_gain.reshape(1, D),
    )


def shards(
    tokens,
    queries,
    keys,
    values,
    neighbours,
    live_bits,
    out_proj,
    norm_gain,
    router,
    expert,
    slot,
    w_up,
    w_down,
):
    tok_dev = tokens.shape[0]
    tiles_dev = tok_dev // TILE
    experts = router.shape[1]
    cap = 2 * tok_dev // experts
    my_node = lax.axis_index("node")
    column_count = lax.axis_size("expert")
    owner_node = neighbours // tiles_dev // column_count
    partner = my_node + 1 - 2 * (my_node % 2)
    block_of = jnp.where(owner_node == my_node, 0, jnp.where(owner_node == partner, 1, 2))
    position = block_of * tiles_dev + neighbours % tiles_dev
    hidden, normed = attention_block(
        tokens, queries, keys, values, position, live_bits, out_proj, norm_gain
    )
    logits = jnp.dot(normed, router, preferred_element_type=jnp.float32)
    columns = lax.iota(jnp.int32, experts)
    chosen = jnp.sum(jnp.where(columns[None, :] == expert[:, None], logits, 0.0), axis=-1)
    gate = jax.nn.sigmoid(chosen)
    slot_cell = expert * cap + slot
    one_hot = (lax.iota(jnp.int32, experts * cap)[:, None] == slot_cell[None, :]).astype(
        jnp.bfloat16
    )
    outgoing = jnp.dot(one_hot, normed, preferred_element_type=jnp.float32).astype(jnp.bfloat16)
    up_matrix = w_up[0]
    down_matrix = w_down[0]
    block = lax.all_to_all(
        outgoing.reshape(experts, 1, cap, D),
        ("node", "expert"),
        split_axis=0,
        concat_axis=1,
        tiled=True,
    )
    token_rows = block.reshape(-1, D)
    lifted = jnp.dot(token_rows, up_matrix, preferred_element_type=jnp.float32)
    lifted = jax.nn.gelu(lifted, approximate=True).astype(jnp.bfloat16)
    result = jnp.dot(lifted, down_matrix, preferred_element_type=jnp.float32).astype(jnp.bfloat16)
    returned = lax.all_to_all(
        result.reshape(block.shape), ("node", "expert"), split_axis=1, concat_axis=0, tiled=True
    )
    flat_back = returned.reshape(experts * cap, D)
    expert_out = jnp.einsum("ct,cd->td", one_hot, flat_back, preferred_element_type=jnp.float32)
    layer_out = hidden + gate[:, None] * expert_out
    return layer_out.astype(jnp.bfloat16)


def solution(mesh):
    in_specs = (
        P(("node", "expert"), None),
        P(("node", "expert"), None),
        P(("node", "expert"), None),
        P(("node", "expert"), None),
        P(("node", "expert"), None),
        P(("node", "expert"), None),
        P(),
        P(),
        P(),
        P(("node", "expert")),
        P(("node", "expert")),
        P(("node", "expert"), None, None),
        P(("node", "expert"), None, None),
    )
    out_specs = P(("node", "expert"), None)
    return jax.shard_map(shards, mesh=mesh, in_specs=in_specs, out_specs=out_specs, check_vma=False)
```

time: 356 us -> 221 us (0.62)
  waiting for transfers between devices: 129 us -> 48.2 us
  local copies, waits for them, and re-layouts: 84.3 us -> 5.66 us
  Pallas kernels: 0 us -> 76.8 us
  matrix products: 69.1 us -> 30.5 us
  starting transfers between devices: 9.8 us -> 3.67 us
  other arithmetic: 7.34 us -> 2.13 us
    ppermute x2 -> x0, waiting for transfers between devices: 82.3 us -> none  [the longest x1 82.2 us: extended(): after = lax.ppermute(leading, axis, down)]
    pallas_call x0 -> x1, Pallas kernels: none -> 76.8 us  [attention_block(): pl.pallas_call(functools.partial(attention_kernel, lax.axis_size('node'))...]
    slice x3 -> x0, local copies, waits for them, and re-layouts: 36.5 us -> none  [the longest x2 24.2 us: shards(): near_keys = gathered[..., :D].reshape(tiles_dev, NB * TILE, HEADS, HEAD_DIM)]
    reshape x3 -> x0, local copies, waits for them, and re-layouts: 30.6 us -> none  [the longest x1 13.3 us: shards(): gathered[..., D:].reshape(tiles_dev, NB * TILE, HEADS, HEAD_DIM)]
    sub x1 -> x0, matrix products: 18.8 us -> none  [shards(): weights = jnp.exp(masked - peak)]
    dot_general x2 -> x0, matrix products: 17.3 us -> none  [the longest x1 14.7 us: shards(): jnp.einsum('thqk,tkhd->tqhd', weights, near_values, preferred_element_typ...]
    gather x1 -> x0, local copies, waits for them, and re-layouts: 10 us -> none  [shards(): gathered = window_tiles[position]]
    ppermute x2 -> x0, starting transfers between devices: 6.01 us -> none  [the longest x1 6.01 us: extended(): after = lax.ppermute(leading, axis, down)]
  transfers between devices with their start and end apart: 3 -> 1, of which waited for: 3 -> 1; matrix products, arithmetic and copies ran while one was open for 2% -> 0% of each run, Pallas kernels for 0% -> 0%
where the time goes in v1:
time: 221 us; the launch traced here: 220 us
  Pallas kernels  76.8 us (35%)
  blocking collectives  53.1 us (24%)
  waiting for transfers between devices  48.2 us (22%)
  matrix products  30.5 us (14%)
  local copies, waits for them, and re-layouts  5.66 us (3%)
  starting transfers between devices  3.67 us (2%)
    pallas_call x1, Pallas kernels, attention_block(): pl.pallas_call(functools.partial(attention_kernel, lax.axis_size('node'))...  76.8 us
    all_to_all x1, blocking collectives, shards(): lax.all_to_all(outgoing.reshape(experts, 1, cap, D), ('node', 'expert'),...  53.1 us
    all_to_all x1, waiting for transfers between devices, shards(): lax.all_to_all(result.reshape(block.shape), ('node', 'expert'), split_axi...  48.2 us
    dot_general x1, matrix products, shards(): jnp.dot(lifted, down_matrix, preferred_element_type=jnp.float32)  25 us
    unnamed x14, local copies, waits for them, and re-layouts  5.59 us
  transfers between devices with their start and end apart: 1, of which 1 were waited for; matrix products, arithmetic and copies ran while one was open for 0% of the time, Pallas kernels for 0%

profile of v1, /device:TPU:0, one launch (start us, length us, event | category | flops | bytes accessed | tf_op | source)
XLA Modules:
  0.0 220.2 jit_solution(332628023448927363)
XLA Ops:
  0.0 0.0 copy-start
  0.0 0.7 compare_select_fusion
  0.7 0.7 fusion.32.position_ref
  1.4 0.7 multiply_add_fusion
  2.1 0.1 broadcast_in_dim.28
  2.2 0.0 copy-start.1
  2.2 1.2 copy-done.1
  3.4 0.0 copy-start.2
  3.4 1.2 copy-done.2
  4.6 0.0 copy-start.3
  4.6 1.2 copy-done.3
  5.9 0.0 copy-start.4
  5.9 1.2 copy-done.4
  7.1 0.7 copy-done.5
  7.8 76.8 %shard_map.127 = (f32[512,1024]{1,0:T(8,128)}, bf16[512,1024]{1,0:T(8,128)(2,1)S(1)}) custom-call(s32[4,8]{1,0:T(4,128)S(1)} %fusion.32.position_ref, f32[4,1,1024]{2,1,0:T(1,128)S(1)} %bitcast.31, bf16[512,1024]{1,0:T(8,128)(2,1)S(1)} %copy-done.1, bf16[4,128,1024]{2,1,0:T(8,128)(2,1)S(1)} %bitcast.29, bf16[4,128,1024]{2,1,0:T(8,128)(2,1)S(1)} %bitcast.30, ...), custom_call_target="tpu_custom_call" | custom-call | tf_op jit(solution)/shard_map/pallas_call | solution.py:169
  84.6 1.3 fusion.27
  85.9 53.1 %all_to_all.8 = bf16[32,1,32,1024]{3,2,1,0:T(8,128)(2,1)S(1)} all-to-all(bf16[32,1,32,1024]{3,2,1,0:T(8,128)(2,1)S(1)} %bitcast.36), channel_id=1, replica_groups=mesh['node'=8,'expert'=4] {'node','expert'}, dimensions={0} | all-to-all | bytes 4194304 | tf_op jit(solution)/shard_map/all_to_all | solution.py:243
  139.0 25.0 %fusion.18 = bf16[1024,1024]{1,0:T(8,128)(2,1)} fusion(bf16[1,4096,1024]{2,1,0:T(8,128)(2,1)} %param.25, bf16[1024,1024]{1,0:T(8,128)(2,1)S(1)} %bitcast.35, bf16[1,1024,4096]{2,1,0:T(8,128)(2,1)} %param.24), kind=kOutput, calls=%fused_computation.20 | convolution fusion | flops 17218666496 | bytes 20971520 | tf_op jit(solution)/shard_map/dot_general | solution.py:253
  163.9 3.7 %all-to-all-start.1 = ((bf16[1,32,32,1024]{3,2,0,1:T(8,128)(2,1)}), bf16[1,32,32,1024]{3,2,0,1:T(8,128)(2,1)S(1)}, u32[]{:S(2)}, u32[]{:S(2)}) async-start(bf16[1,32,32,1024]{3,2,0,1:T(8,128)(2,1)} %bitcast.34), calls=%async_computation.1 | async-start | bytes 4194304 | tf_op jit(solution)/shard_map/all_to_all | solution.py:254
  167.6 0.0 copy-done
  167.6 0.0 copy-done.6
  167.6 0.4 fusion.28
  168.1 48.2 %all-to-all-done.1 = bf16[1,32,32,1024]{3,2,0,1:T(8,128)(2,1)S(1)} async-done(((bf16[1,32,32,1024]{3,2,0,1:T(8,128)(2,1)}), bf16[1,32,32,1024]{3,2,0,1:T(8,128)(2,1)S(1)}, u32[]{:S(2)}, u32[]{:S(2)}) %all-to-all-start.1) | async-done | bytes 2097184 | tf_op jit(solution)/shard_map/all_to_all | solution.py:254
  216.3 3.9 %add_convert_fusion = bf16[512,1024]{1,0:T(8,128)(2,1)} fusion(f32[512,1024]{1,0:T(8,128)} %get-tuple-element.7, bf16[1024,1024]{1,0:T(8,128)(2,1)S(1)} %bitcast.33, s32[512]{0:T(512)S(1)} %multiply_add_fusion, f32[512]{0:T(512)S(1)} %add_divide_fusion), kind=kOutput, calls=%fused_computation.16 | convolution fusion | flops 1075838976 | bytes 5246976 | tf_op jit(solution)/shard_map/ct,cd->td/dot_general | solution.py:258
  (3 shorter events, 0.0 us)
Async XLA Ops:
  0.0 167.6 %copy-start = (bf16[1024,32]{0,1:T(8,128)(2,1)S(1)}, bf16[1024,32]{0,1:T(8,128)(2,1)}, u32[]{:S(2)}) copy-start(bf16[1024,32]{0,1:T(8,128)(2,1)} %param.21) | copy-start | bytes 196612
  2.2 1.2 copy-start.1
  3.4 1.2 copy-start.2
  4.6 1.2 copy-start.3
  5.9 1.2 copy-start.4
  7.1 0.7 copy-start.5
  163.9 3.7 %copy-start.6 = (s32[512]{0:T(512)S(1)}, s32[512]{0:T(512)}, u32[]{:S(2)}) copy-start(s32[512]{0:T(512)} %param.22) | copy-start | bytes 6148
  163.9 52.4 %all-to-all-start.1 = ((bf16[1,32,32,1024]{3,2,0,1:T(8,128)(2,1)}), bf16[1,32,32,1024]{3,2,0,1:T(8,128)(2,1)S(1)}, u32[]{:S(2)}, u32[]{:S(2)}) async-start(bf16[1,32,32,1024]{3,2,0,1:T(8,128)(2,1)} %bitcast.34), calls=%async_computation.1 | async-start | bytes 4194304 | tf_op jit(solution)/shard_map/all_to_all | solution.py:254

commit v2 on v1

--- a/solution.py
+++ b/solution.py
@@ -19,24 +19,29 @@
 
 CHUNKS = 4
 HIDE = -1e30
+STACK = 2
 
 
 def attention_kernel(
     nodes,
     position_ref,
     bias_ref,
-    query_ref,
+    query_hbm,
     key_ref,
     value_ref,
-    token_ref,
-    proj_ref,
+    token_hbm,
+    proj_hbm,
     gain_ref,
     hidden_ref,
     normed_ref,
     *scratch,
 ):
     key_windows, value_windows = scratch[:CHUNKS], scratch[CHUNKS : 2 * CHUNKS]
-    own_sem, x_send, x_recv, z_send, z_recv, attn_ref = scratch[2 * CHUNKS :]
+    own_sem, x_send, x_recv, z_send, z_recv, attn_ref = scratch[2 * CHUNKS : 2 * CHUNKS + 6]
+    query_ref, token_ref, proj_ref, load_sem = scratch[2 * CHUNKS + 6 :]
+    token_load = pltpu.make_async_copy(token_hbm, token_ref, load_sem.at[0])
+    query_load = pltpu.make_async_copy(query_hbm, query_ref, load_sem.at[1])
+    proj_load = pltpu.make_async_copy(proj_hbm, proj_ref, load_sem.at[2])
     node = lax.axis_index("node")
     odd = node % 2
     partner = node + 1 - 2 * odd
@@ -82,8 +87,9 @@
             )
     for copy in first:
         copy.start()
-    for copy in own:
+    for copy in own + [token_load, query_load, proj_load]:
         copy.start()
+    token_load.wait()
     hidden_ref[...] = token_ref[...].astype(jnp.float32)
     heads = width // HEAD_DIM
     lane_head = lax.broadcasted_iota(jnp.int32, (TILE, width), 1) // HEAD_DIM
@@ -105,8 +111,14 @@
             )
             bias = bias_ref[t]
             mixed = jnp.zeros((TILE, width), jnp.float32)
-            for h in range(heads):
-                mine = jnp.where(lane_head == h, query, jnp.zeros_like(query))
+            for h in range(0, heads, STACK):
+                mine = jnp.concatenate(
+                    [
+                        jnp.where(lane_head == h + i, query, jnp.zeros_like(query))
+                        for i in range(STACK)
+                    ],
+                    axis=0,
+                )
                 scores = lax.dot_general(
                     mine,
                     near_keys,
@@ -119,7 +131,8 @@
                 share = 1.0 / jnp.sum(weights, axis=-1, keepdims=True)
                 weights = (weights * share).astype(jnp.bfloat16)
                 out = jnp.dot(weights, near_values, preferred_element_type=jnp.float32)
-                mixed = jnp.where(lane_head == h, out, mixed)
+                for i in range(STACK):
+                    mixed = jnp.where(lane_head == h + i, out[i * TILE : (i + 1) * TILE], mixed)
             attn_ref[rows, :] = mixed.astype(jnp.bfloat16)
             return carry
 
@@ -136,6 +149,8 @@
 
         lax.fori_loop(0, tiles, project, 0)
 
+    query_load.wait()
+    proj_load.wait()
     relay(0)
     for c in range(CHUNKS):
         if c + 1 < CHUNKS:
@@ -166,6 +181,7 @@
     window = pltpu.VMEM((3 * tiles, TILE, width), jnp.bfloat16)
     sems = pltpu.SemaphoreType.DMA((2 * CHUNKS,))
     vmem = pl.BlockSpec(memory_space=pltpu.VMEM)
+    anywhere = pl.BlockSpec(memory_space=pl.ANY)
     return pl.pallas_call(
         functools.partial(attention_kernel, lax.axis_size("node")),
         out_shape=(
@@ -175,19 +191,25 @@
         in_specs=[
             pl.BlockSpec(memory_space=pltpu.SMEM),
             vmem,
-            vmem,
-            pl.BlockSpec(memory_space=pl.ANY),
-            pl.BlockSpec(memory_space=pl.ANY),
-            vmem,
-            vmem,
+            anywhere,
+            anywhere,
+            anywhere,
+            anywhere,
+            anywhere,
             vmem,
         ],
         out_specs=(vmem, vmem),
         scratch_shapes=[window] * (2 * CHUNKS)
         + [sems] * 5
-        + [pltpu.VMEM((tok_dev, width), jnp.bfloat16)],
+        + [
+            pltpu.VMEM((tok_dev, width), jnp.bfloat16),
+            pltpu.VMEM((tok_dev, D), jnp.bfloat16),
+            pltpu.VMEM((tok_dev, D), jnp.bfloat16),
+            pltpu.VMEM((D, D), jnp.bfloat16),
+            pltpu.SemaphoreType.DMA((3,)),
+        ],
         compiler_params=pltpu.CompilerParams(
-            collective_id=0, has_side_effects=True, vmem_limit_bytes=48 * 1024 * 1024
+            collective_id=0, has_side_effects=True, vmem_limit_bytes=62 * 1024 * 1024
         ),
     )(
         position,
@@ -198,6 +220,185 @@
         tokens,
         out_proj,
         norm_gain.reshape(1, D),
+    )
+
+
+GROUPS = 4
+SPAN = 512
+
+
+def expert_kernel(
+    nodes, columns, outgoing_ref, up_ref, down_ref, back_ref, *scratch
+):
+    (
+        rows_ref,
+        result_ref,
+        up_held,
+        down_held,
+        total_ref,
+        weight_sem,
+        own_sem,
+        there_send,
+        there_recv,
+        back_send,
+        back_recv,
+    ) = scratch
+    devices = nodes * columns
+    cap = outgoing_ref.shape[1]
+    members = devices // GROUPS
+    me = lax.axis_index("node") * columns + lax.axis_index("expert")
+    up_copy = pltpu.make_async_copy(up_ref.at[0], up_held, weight_sem.at[0])
+    down_copy = pltpu.make_async_copy(down_ref.at[0], down_held, weight_sem.at[1])
+
+    def place(device):
+        return {"node": device // columns, "expert": device % columns}
+
+    barrier = pltpu.get_barrier_semaphore()
+
+    def greet(k, carry):
+        pl.semaphore_signal(
+            barrier,
+            inc=1,
+            device_id=place((me + k) % devices),
+            device_id_type=pl.DeviceIdType.MESH,
+        )
+        return carry
+
+    lax.fori_loop(1, devices, greet, 0)
+    pl.semaphore_wait(barrier, devices - 1)
+
+    def block(g, j):
+        return pl.ds(pl.multiple_of(j * cap, cap), cap)
+
+    def there(i):
+        g, j = i // members, i % members
+        target = (me + g + GROUPS * j) % devices
+        return pltpu.make_async_remote_copy(
+            src_ref=outgoing_ref.at[target],
+            dst_ref=rows_ref.at[g, block(g, j)],
+            send_sem=there_send.at[i],
+            recv_sem=there_recv.at[i],
+            device_id=place(target),
+            device_id_type=pl.DeviceIdType.MESH,
+        )
+
+    def back(i):
+        g, j = i // members, i % members
+        target = (me + devices - g - GROUPS * j) % devices
+        return pltpu.make_async_remote_copy(
+            src_ref=result_ref.at[g, block(g, j)],
+            dst_ref=back_ref.at[me],
+            send_sem=back_send.at[i],
+            recv_sem=back_recv.at[i],
+            device_id=place(target),
+            device_id_type=pl.DeviceIdType.MESH,
+        )
+
+    def back_from(i):
+        g, j = i // members, i % members
+        source = (me + g + GROUPS * j) % devices
+        return pltpu.make_async_remote_copy(
+            src_ref=result_ref.at[g, block(g, j)],
+            dst_ref=back_ref.at[source],
+            send_sem=back_send.at[i],
+            recv_sem=back_recv.at[i],
+            device_id=place(source),
+            device_id_type=pl.DeviceIdType.MESH,
+        )
+
+    def each(lower, upper, act):
+        def step(i, carry):
+            act(i)
+            return carry
+
+        lax.fori_loop(lower, upper, step, 0)
+
+    each(1, devices, lambda i: there(i).start())
+    up_copy.start()
+    down_copy.start()
+    own_rows = pltpu.make_async_copy(
+        outgoing_ref.at[me], rows_ref.at[0, pl.ds(0, cap)], own_sem.at[0]
+    )
+    own_rows.start()
+    own_back = pltpu.make_async_copy(
+        result_ref.at[0, pl.ds(0, cap)], back_ref.at[me], own_sem.at[1]
+    )
+    spans = up_held.shape[1] // SPAN
+    for g in range(GROUPS):
+        first = max(g * members, 1)
+        each(first, (g + 1) * members, lambda i: there(i).wait_recv())
+        if g == 0:
+            own_rows.wait()
+            up_copy.wait()
+            down_copy.wait()
+
+        def span(f, carry, g=g):
+            part = pl.ds(pl.multiple_of(f * SPAN, SPAN), SPAN)
+            lifted = jnp.dot(rows_ref[g], up_held[:, part], preferred_element_type=jnp.float32)
+            lifted = jax.nn.gelu(lifted, approximate=True).astype(jnp.bfloat16)
+            total_ref[...] += jnp.dot(
+                lifted, down_held[part, :], preferred_element_type=jnp.float32
+            )
+            return carry
+
+        total_ref[...] = jnp.zeros_like(total_ref)
+        lax.fori_loop(0, spans, span, 0)
+        result_ref[g] = total_ref[...].astype(jnp.bfloat16)
+        if g == 0:
+            own_back.start()
+        each(first, (g + 1) * members, lambda i: back(i).start())
+    own_back.wait()
+    each(1, devices, lambda i: there(i).wait_send())
+    each(1, devices, lambda i: back(i).wait_send())
+    each(1, devices, lambda i: back_from(i).wait_recv())
+
+
+def expert_exchange(outgoing, w_up, w_down):
+    devices, cap, _ = outgoing.shape
+    hidden_units = w_up.shape[2]
+    rows = devices // GROUPS * cap
+    anywhere = pl.BlockSpec(memory_space=pl.ANY)
+    sems = pltpu.SemaphoreType.DMA((devices,))
+    pair = pltpu.SemaphoreType.DMA((2,))
+    return pl.pallas_call(
+        functools.partial(expert_kernel, lax.axis_size("node"), lax.axis_size("expert")),
+        out_shape=jax.ShapeDtypeStruct(outgoing.shape, jnp.bfloat16),
+        in_specs=[anywhere] * 3,
+        out_specs=anywhere,
+        scratch_shapes=[
+            pltpu.VMEM((GROUPS, rows, D), jnp.bfloat16),
+            pltpu.VMEM((GROUPS, rows, D), jnp.bfloat16),
+            pltpu.VMEM((D, hidden_units), jnp.bfloat16),
+            pltpu.VMEM((hidden_units, D), jnp.bfloat16),
+            pltpu.VMEM((rows, D), jnp.float32),
+            pair,
+            pair,
+            sems,
+            sems,
+            sems,
+            sems,
+        ],
+        compiler_params=pltpu.CompilerParams(
+            collective_id=1, has_side_effects=True, vmem_limit_bytes=62 * 1024 * 1024
+        ),
+    )(outgoing, w_up, w_down)
+
+
+def exchange_by_blocks(outgoing, w_up, w_down):
+    experts, cap, _ = outgoing.shape
+    block = lax.all_to_all(
+        outgoing.reshape(experts, 1, cap, D),
+        ("node", "expert"),
+        split_axis=0,
+        concat_axis=1,
+        tiled=True,
+    )
+    token_rows = block.reshape(-1, D)
+    lifted = jnp.dot(token_rows, w_up[0], preferred_element_type=jnp.float32)
+    lifted = jax.nn.gelu(lifted, approximate=True).astype(jnp.bfloat16)
+    result = jnp.dot(lifted, w_down[0], preferred_element_type=jnp.float32).astype(jnp.bfloat16)
+    return lax.all_to_all(
+        result.reshape(block.shape), ("node", "expert"), split_axis=1, concat_axis=0, tiled=True
     )
 
 
@@ -238,22 +439,8 @@
         jnp.bfloat16
     )
     outgoing = jnp.dot(one_hot, normed, preferred_element_type=jnp.float32).astype(jnp.bfloat16)
-    up_matrix = w_up[0]
-    down_matrix = w_down[0]
-    block = lax.all_to_all(
-        outgoing.reshape(experts, 1, cap, D),
-        ("node", "expert"),
-        split_axis=0,
-        concat_axis=1,
-        tiled=True,
-    )
-    token_rows = block.reshape(-1, D)
-    lifted = jnp.dot(token_rows, up_matrix, preferred_element_type=jnp.float32)
-    lifted = jax.nn.gelu(lifted, approximate=True).astype(jnp.bfloat16)
-    result = jnp.dot(lifted, down_matrix, preferred_element_type=jnp.float32).astype(jnp.bfloat16)
-    returned = lax.all_to_all(
-        result.reshape(block.shape), ("node", "expert"), split_axis=1, concat_axis=0, tiled=True
-    )
+    exchange = exchange_by_blocks if cap % 16 else expert_exchange
+    returned = exchange(outgoing.reshape(experts, cap, D), w_up, w_down)
     flat_back = returned.reshape(experts * cap, D)
     expert_out = jnp.einsum("ct,cd->td", one_hot, flat_back, preferred_element_type=jnp.float32)
     layer_out = hidden + gate[:, None] * expert_out

time: 221 us -> 180 us (0.81)
  Pallas kernels: 76.8 us -> 166 us
  blocking collectives: 53.1 us -> 0 us
  waiting for transfers between devices: 48.2 us -> 0 us
  matrix products: 30.5 us -> 9.95 us
  local copies, waits for them, and re-layouts: 5.66 us -> 0.69 us
  starting transfers between devices: 3.67 us -> 0 us
    pallas_call x0 -> x1, Pallas kernels: none -> 97.4 us  [expert_exchange(): pl.pallas_call(functools.partial(expert_kernel, lax.axis_size('node'), la...]
    all_to_all x1 -> x0, blocking collectives: 53.1 us -> none  [shards(): lax.all_to_all(outgoing.reshape(experts, 1, cap, D), ('node', 'expert'),...]
    all_to_all x1 -> x0, waiting for transfers between devices: 48.2 us -> none  [shards(): lax.all_to_all(result.reshape(block.shape), ('node', 'expert'), split_axi...]
    dot_general x1 -> x0, matrix products: 25 us -> none  [shards(): jnp.dot(lifted, down_matrix, preferred_element_type=jnp.float32)]
    pallas_call x1, Pallas kernels: 76.8 us -> 69 us  [attention_block(): pl.pallas_call(functools.partial(attention_kernel, lax.axis_size('node'))...]
    unnamed x14 -> x4, local copies, waits for them, and re-layouts: 5.59 us -> 0.01 us
    all_to_all x1 -> x0, starting transfers between devices: 3.67 us -> none  [shards(): lax.all_to_all(result.reshape(block.shape), ('node', 'expert'), split_axi...]
    dot_general x1, matrix products: 1.26 us -> 3.79 us  [shards(): jnp.dot(one_hot, normed, preferred_element_type=jnp.float32)]
  transfers between devices with their start and end apart: 1 -> 0, of which waited for: 1 -> 0; matrix products, arithmetic and copies ran while one was open for 0% -> 0% of each run, Pallas kernels for 0% -> 0%
where the time goes in v2:
time: 180 us
  Pallas kernels  166 us (92%)
  matrix products  9.95 us (6%)
  other arithmetic  2.7 us (2%)
    pallas_call x1, Pallas kernels, expert_exchange(): pl.pallas_call(functools.partial(expert_kernel, lax.axis_size('node'), la...  97.4 us
    pallas_call x1, Pallas kernels, attention_block(): pl.pallas_call(functools.partial(attention_kernel, lax.axis_size('node'))...  69 us
    dot_general x1, matrix products, shards(): jnp.einsum('ct,cd->td', one_hot, flat_back, preferred_element_type=jnp.fl...  4.5 us
    dot_general x1, matrix products, shards(): jnp.dot(one_hot, normed, preferred_element_type=jnp.float32)  3.79 us

profile of v2, /device:TPU:0, one launch (start us, length us, event | category | flops | bytes accessed | tf_op | source)
XLA Modules:
  0.0 179.8 jit_solution(13316737139598363191)
XLA Ops:
  0.0 0.0 copy-start
  0.0 1.3 fusion.7.position_ref
  1.3 0.7 multiply_add_fusion
  2.0 0.7 compare_select_fusion
  2.7 0.7 broadcast_in_dim.28
  3.4 0.0 copy-start.1
  3.4 69.0 %shard_map.127 = (f32[512,1024]{1,0:T(8,128)}, bf16[512,1024]{1,0:T(8,128)(2,1)}) custom-call(s32[4,8]{1,0:T(4,128)} %fusion.7.position_ref, f32[4,1,1024]{2,1,0:T(1,128)} %bitcast.14, bf16[512,1024]{1,0:T(8,128)(2,1)} %query_hbm.1, bf16[4,128,1024]{2,1,0:T(8,128)(2,1)} %bitcast.12, bf16[4,128,1024]{2,1,0:T(8,128)(2,1)} %bitcast.13, ...), custom_call_target="tpu_custom_call" | custom-call | tf_op jit(solution)/shard_map/pallas_call | solution.py:185
  72.4 0.0 copy-done
  72.4 0.0 copy-done.1
  72.4 1.7 fusion.3
  74.1 3.8 %fusion.2 = bf16[1024,1024]{1,0:T(8,128)(2,1)} fusion(bf16[512,1024]{1,0:T(8,128)(2,1)} %get-tuple-element.8, s32[512]{0:T(512)S(1)} %multiply_add_fusion), kind=kOutput, calls=%fused_computation.4 | convolution fusion | flops 1075314688 | bytes 3147776 | tf_op jit(solution)/shard_map/dot_general | solution.py:441
  77.8 97.4 %shard_map.128 = bf16[32,32,1024]{2,1,0:T(8,128)(2,1)} custom-call(bf16[32,32,1024]{2,1,0:T(8,128)(2,1)} %bitcast.11, bf16[1,1024,4096]{2,1,0:T(8,128)(2,1)} %up_ref.1, bf16[1,4096,1024]{2,1,0:T(8,128)(2,1)} %down_ref.1), custom_call_target="tpu_custom_call" | custom-call | tf_op jit(solution)/shard_map/pallas_call | solution.py:363
  175.3 4.5 %add_convert_fusion = bf16[512,1024]{1,0:T(8,128)(2,1)} fusion(f32[512,1024]{1,0:T(8,128)} %get-tuple-element.7, bf16[1024,1024]{1,0:T(8,128)(2,1)} %bitcast.10, s32[512]{0:T(512)S(1)} %multiply_add_fusion, f32[512]{0:T(512)S(1)} %add_divide_fusion), kind=kOutput, calls=%fused_computation | convolution fusion | flops 1075838976 | bytes 5246976 | tf_op jit(solution)/shard_map/ct,cd->td/dot_general | solution.py:445
  (1 shorter events, 0.0 us)
Async XLA Ops:
  0.0 72.4 %copy-start = (bf16[1024,32]{0,1:T(8,128)(2,1)S(1)}, bf16[1024,32]{0,1:T(8,128)(2,1)}, u32[]{:S(2)}) copy-start(bf16[1024,32]{0,1:T(8,128)(2,1)} %param.21) | copy-start | bytes 196612
  3.4 69.0 %copy-start.1 = (s32[512]{0:T(512)S(1)}, s32[512]{0:T(512)}, u32[]{:S(2)}) copy-start(s32[512]{0:T(512)} %param.22) | copy-start | bytes 6148
